TPU v7x, 32 devices: a 4x4x1 block of a 4x4x8 slice. The times are simulated.
32 devices in a mesh: dp: 1 (over z), ep: 32 (over y, x, core).
Axes of the slice: x: 4, y: 4, z: 1, core: 2. Of those that a mesh axis runs over, the one named last changes fastest.
The devices are a block of a 4x4x8 slice.
Arguments:
- tokens: bfloat16 [8192, 1024], P(('dp', 'ep'))
- expert_ids: int32 [8192, 8], P(('dp', 'ep'))
- gate_w: float32 [8192, 8], P(('dp', 'ep'))
- route_counts: int32 [32, 32], P(('dp', 'ep'))
- w_gate: bfloat16 [32, 1024, 512], P('ep')
- w_up: bfloat16 [32, 1024, 512], P('ep')
- w_down: bfloat16 [32, 512, 1024], P('ep')
Outputs:
- output: bfloat16 [8192, 1024], P(('dp', 'ep'))
All inputs are finite; a program needn't handle non-finite values.
Results may differ from a plain program's by a relative error of at most 0.00360921.
Values are sent between devices in bfloat16 or wider.
A program may use at most 768 MiB of HBM per device.

v0:
```python
import jax
import jax.numpy as jnp
from jax import lax
from jax.sharding import PartitionSpec as P


def place_rows(expert_ids, counts_row, cap_rows, n_exp):
    tok_n, top_n = expert_ids.shape
    flat_ids = expert_ids.reshape(tok_n * top_n)
    onehot = (flat_ids[:, None] == jnp.arange(n_exp)[None, :]).astype(jnp.int32)
    before = jnp.cumsum(onehot, axis=0) - onehot
    slot_idx = jnp.sum(before * onehot, axis=1)
    row_limit = jnp.sum(onehot * counts_row[None, :], axis=1)
    buf_pos = jnp.where(slot_idx < row_limit, flat_ids * cap_rows + slot_idx, -1)
    return buf_pos.reshape(tok_n, top_n)


def expert_ffn(rows_in, w_gate, w_up, w_down):
    act_a = jnp.einsum("erd,edf->erf", rows_in, w_gate, preferred_element_type=jnp.float32)
    act_b = jnp.einsum("erd,edf->erf", rows_in, w_up, preferred_element_type=jnp.float32)
    hidden = (jax.nn.silu(act_a) * act_b).astype(jnp.bfloat16)
    return jnp.einsum("erf,efd->erd", hidden, w_down, preferred_element_type=jnp.float32).astype(jnp.bfloat16)


def solution(mesh):
    group_size = mesh.shape["ep"]
    row_spec = P(("dp", "ep"))

    def local_step(tokens, expert_ids, gate_w, route_counts, w_gate, w_up, w_down):
        tok_n = expert_ids.shape[0]
        n_local = w_gate.shape[0]
        model_dim = w_gate.shape[1]
        n_exp = n_local * group_size
        cap_rows = tok_n // 2
        buf_pos = place_rows(expert_ids, route_counts[0], cap_rows, n_exp)
        disp_mat = jnp.any(jnp.arange(n_exp * cap_rows)[:, None, None] == buf_pos[None, :, :], axis=2).astype(jnp.bfloat16)
        packed = jnp.dot(disp_mat, tokens, preferred_element_type=jnp.float32).astype(jnp.bfloat16)
        packed = packed.reshape(group_size, n_local, cap_rows, model_dim)
        arrived = lax.all_to_all(packed, "ep", 0, 2, tiled=True)
        expert_out = expert_ffn(arrived.reshape(n_local, group_size * cap_rows, model_dim), w_gate, w_up, w_down)
        returned = lax.all_to_all(expert_out.reshape(1, n_local, group_size * cap_rows, model_dim), "ep", 2, 0, tiled=True)
        picked = jnp.take(returned.reshape(n_exp * cap_rows, model_dim), jnp.maximum(buf_pos, 0), axis=0)
        weights = jnp.where(buf_pos >= 0, gate_w, 0.0)
        total_f32 = tokens.astype(jnp.float32) + jnp.sum(weights[:, :, None] * picked.astype(jnp.float32), axis=1)
        return total_f32.astype(jnp.bfloat16)

    return jax.shard_map(local_step, mesh=mesh, in_specs=(row_spec, row_spec, row_spec, row_spec, P("ep"), P("ep"), P("ep")), out_specs=row_spec, check_vma=False)
```

profile of v0, /device:TPU:103, one launch (start us, length us, event | category | flops | bytes accessed | tf_op | source)
XLA Modules:
  0.0 452.2 jit_solution(2651039520451150592)
XLA Ops:
  0.0 0.9 copy.54
  1.2 9.1 %reduce-window.6 = s32[32,16,128]{2,1,0:T(8,128)S(1)} reduce-window(s32[32,16,128]{2,1,0:T(8,128)S(1)} %fusion.10, s32[]{:T(128)} %constant.15.clone.1), window={size=1x1x128 pad=0_0x0_0x127_0}, to_apply=%region_0.0 | reduce-window | flops 8323072 | bytes 524292 | tf_op jit(solution)/shard_map/reduce-window
  10.4 0.2 copy.66
  10.6 0.2 reduce-window.9
  11.0 0.8 select_reduce_fusion
  12.1 0.7 broadcast_compare_fusion
  12.8 37.4 %fusion = pred[4096,256]{1,0:T(8,128)(4,1)S(1)} fusion(s32[256,8]{0,1:T(8,128)S(1)} %get-tuple-element.8), kind=kLoop, calls=%fused_computation.2 | loop fusion | flops 15728640 | bytes 1056768 | tf_op jit(solution)/shard_map/reduce_or | solution.py:36
  50.2 3.4 convolution_convert_fusion
  53.6 108.5 %all_to_all.8 = bf16[32,1,128,1024]{3,2,1,0:T(8,128)(2,1)S(1)} all-to-all(bf16[32,1,128,1024]{3,2,1,0:T(8,128)(2,1)S(1)} %bitcast.57), channel_id=1, replica_groups=mesh['dp'=1,'ep'=32] {'ep'}, dimensions={0} | all-to-all | bytes 16777216 | tf_op jit(solution)/shard_map/all_to_all | solution.py:39
  162.2 3.2 copy-done.2
  165.4 6.8 %fusion.5 = f32[4096,512]{1,0:T(8,128)} fusion(bf16[4096,1024]{1,0:T(8,128)(2,1)S(1)} %bitcast.55, bf16[1,1024,512]{2,1,0:T(8,128)(2,1)S(1)} %copy-done.5), kind=kOutput, calls=%fused_computation.12 | convolution fusion | flops 4294967296 | bytes 17825792 | tf_op jit(solution)/shard_map/erd,edf->erf/dot_general | solution.py:19
  172.2 15.5 %convert_bitcast_fusion = bf16[1,1,4096,1024]{3,2,1,0:T(8,128)(2,1)} fusion(f32[4096,512]{1,0:T(8,128)} %fusion.5, bf16[4096,1024]{1,0:T(8,128)(2,1)} %bitcast.56, bf16[1,512,1024]{2,1,0:T(8,128)(2,1)S(1)} %copy-done, bf16[1,1024,512]{2,1,0:T(8,128)(2,1)S(1)} %copy-done.6), kind=kOutput, calls=%fused_computation.5 | convolution fusion | flops 8606711808 | bytes 27262976 | tf_op jit(solution)/shard_map/erf,efd->erd/dot_general | solution.py:22
  187.8 15.5 %copy.73 = bf16[1,1,4096,1024]{3,1,0,2:T(2,128)(2,1)} copy(bf16[1,1,4096,1024]{3,2,1,0:T(8,128)(2,1)} %convert_bitcast_fusion) | data formatting | bytes 16777216 | tf_op jit(solution)/shard_map/reshape | solution.py:41
  203.2 0.5 broadcast.49
  203.7 49.5 %reduce = bf16[4096,1024]{1,0:T(8,128)(2,1)} reduce(bf16[4096,1,1,1024]{3,2,1,0:T(2,128)(2,1)} %bitcast.54, bf16[]{:T(256)} %broadcast.49), dimensions={1,2}, to_apply=%bitcast.50.reduce_sub_computation | reduce | bytes 16777218
  253.3 21.6 %reshape.103 = bf16[32,2,65536]{2,1,0:T(2,128)(2,1)} reshape(bf16[4096,1024]{1,0:T(8,128)(2,1)} %reduce) | data formatting | bytes 16777216
  274.8 6.6 %all-to-all-start.1 = ((bf16[32,2,65536]{2,1,0:T(2,128)(2,1)}), bf16[32,2,65536]{2,1,0:T(2,128)(2,1)}, u32[]{:S(2)}, u32[]{:S(2)}) async-start(bf16[32,2,65536]{2,1,0:T(2,128)(2,1)} %reshape.103), calls=%async_computation.1 | async-start | bytes 16777216 | tf_op jit(solution)/shard_map/all_to_all | solution.py:41
  281.8 0.2 copy.62
  282.0 112.7 %all-to-all-done.1 = bf16[32,2,65536]{2,1,0:T(2,128)(2,1)} async-done(((bf16[32,2,65536]{2,1,0:T(2,128)(2,1)}), bf16[32,2,65536]{2,1,0:T(2,128)(2,1)}, u32[]{:S(2)}, u32[]{:S(2)}) %all-to-all-start.1) | async-done | bytes 8388640 | tf_op jit(solution)/shard_map/all_to_all | solution.py:41
  394.7 23.4 %reshape.104 = bf16[4096,1,1,1024]{3,2,1,0:T(2,128)(2,1)} reshape(bf16[32,2,65536]{2,1,0:T(2,128)(2,1)} %all-to-all-done.1) | data formatting | bytes 16777216
  418.1 12.1 %copy.72 = bf16[1,1,4096,1024]{3,2,0,1:T(8,128)(2,1)} copy(bf16[1,1,4096,1024]{3,1,0,2:T(2,128)(2,1)} %bitcast.53) | data formatting | bytes 16777216
  430.2 15.6 %gather_fusion = bf16[2048,1024]{1,0:T(8,128)(2,1)} fusion(bf16[4096,1024]{1,0:T(8,128)(2,1)} %bitcast.52, s32[2048]{0:T(1024)S(1)} %broadcast_clamp_fusion), kind=kCustom, calls=%fused_computation | custom fusion | bytes 8396800 | tf_op jit(solution)/shard_map/jit(_take)/gather | solution.py:42
  445.8 5.4 %multiply_reduce_fusion = f32[256,1024]{1,0:T(8,128)S(1)} fusion(bf16[2048,1024]{1,0:T(8,128)(2,1)} %gather_fusion, f32[256,8]{1,0:T(8,128)S(1)} %copy.61, pred[256,8]{1,0:T(8,128)(4,1)S(1)} %copy.62), kind=kLoop, calls=%fused_computation.4 | loop fusion | flops 8126464 | bytes 5253120 | tf_op jit(solution)/shard_map/reduce_sum | solution.py:44
  451.3 1.0 add_convert_fusion
  (28 shorter events, 1.2 us)
Async XLA Ops:
  0.0 172.2 %copy-start = (bf16[1,512,1024]{2,1,0:T(8,128)(2,1)S(1)}, bf16[1,512,1024]{2,1,0:T(8,128)(2,1)}, u32[]{:S(2)}) copy-start(bf16[1,512,1024]{2,1,0:T(8,128)(2,1)} %param.13) | copy-start | bytes 3145732
  53.6 111.8 %copy-start.5 = (bf16[1,1024,512]{2,1,0:T(8,128)(2,1)S(1)}, bf16[1,1024,512]{2,1,0:T(8,128)(2,1)}, u32[]{:S(2)}) copy-start(bf16[1,1024,512]{2,1,0:T(8,128)(2,1)} %param.11) | copy-start | bytes 3145732
  162.2 3.2 copy-start.2
  165.4 6.9 %copy-start.6 = (bf16[1,1024,512]{2,1,0:T(8,128)(2,1)S(1)}, bf16[1,1024,512]{2,1,0:T(8,128)(2,1)}, u32[]{:S(2)}) copy-start(bf16[1,1024,512]{2,1,0:T(8,128)(2,1)} %param.12) | copy-start | bytes 3145732
  274.8 6.9 %copy-start.4 = (f32[256,8]{0,1:T(8,128)S(1)}, f32[256,8]{0,1:T(8,128)}, u32[]{:S(2)}) copy-start(f32[256,8]{0,1:T(8,128)} %param.9) | copy-start | bytes 24580
  274.8 119.9 %all-to-all-start.1 = ((bf16[32,2,65536]{2,1,0:T(2,128)(2,1)}), bf16[32,2,65536]{2,1,0:T(2,128)(2,1)}, u32[]{:S(2)}, u32[]{:S(2)}) async-start(bf16[32,2,65536]{2,1,0:T(2,128)(2,1)} %reshape.103), calls=%async_computation.1 | async-start | bytes 16777216 | tf_op jit(solution)/shard_map/all_to_all | solution.py:41
  430.2 21.0 %copy-start.3 = (bf16[256,1024]{1,0:T(8,128)(2,1)S(1)}, bf16[256,1024]{1,0:T(8,128)(2,1)}, u32[]{:S(2)}) copy-start(bf16[256,1024]{1,0:T(8,128)(2,1)} %param.7) | copy-start | bytes 1572868
  430.2 22.0 %copy-start.1 = (bf16[1,512,1024]{2,1,0:T(8,128)(2,1)S(1)}, bf16[1,512,1024]{2,1,0:T(8,128)(2,1)}, u32[]{:S(2)}) copy-start(bf16[1,512,1024]{2,1,0:T(8,128)(2,1)} %param.13) | copy-start | bytes 3145732
where the time goes:
time: 454 us; the launch traced here: 452 us
  waiting for transfers between devices  113 us (25%)
  blocking collectives  109 us (24%)
  other arithmetic  104 us (23%)
  local copies, waits for them, and re-layouts  94.1 us (21%)
  matrix products  25.8 us (6%)
  starting transfers between devices  6.61 us (1%)
    all_to_all x1, waiting for transfers between devices, local_step(): lax.all_to_all(expert_out.reshape(1, n_local, group_size * cap_rows, mode...  113 us
    all_to_all x1, blocking collectives, local_step(): arrived = lax.all_to_all(packed, 'ep', 0, 2, tiled=True)  109 us
    unnamed x19, local copies, waits for them, and re-layouts  61.7 us
    unnamed x1, other arithmetic  49.5 us
    reduce_or x1, other arithmetic, local_step(): jnp.any(jnp.arange(n_exp * cap_rows)[:, None, None] == buf_pos[None, :, :...  37.4 us
    gather x1, local copies, waits for them, and re-layouts, local_step(): jnp.take(returned.reshape(n_exp * cap_rows, model_dim), jnp.maximum(buf_p...  15.6 us
    dot_general x1, matrix products, expert_ffn(): jnp.einsum('erf,efd->erd', hidden, w_down, preferred_element_type=jnp.flo...  15.5 us
    reshape x1, local copies, waits for them, and re-layouts, local_step(): expert_out.reshape(1, n_local, group_size * cap_rows, model_dim)  15.5 us
  transfers between devices with their start and end apart: 1, of which 1 were waited for; matrix products, arithmetic and copies ran while one was open for 0% of the time, Pallas kernels for 0%

commit v1 on v0

v1 whole, which is shorter than its diff:
```python
import math

import jax
import jax.numpy as jnp
from jax import lax
from jax.experimental import pallas as pl
from jax.experimental.pallas import tpu as pltpu
from jax.sharding import PartitionSpec as P

MESH = pl.DeviceIdType.MESH
CORES = 2
LANES = 128
CHUNKS = (256, 256, 256, 128, 128)
F32 = jnp.float32
BF16 = jnp.bfloat16


def moe_kernel(side, cols, ids_ref, gate_ref, cnt_ref, tok_hbm, wg_hbm, wu_hbm, wd_hbm, out_ref,
               xbuf, gbuf, gsel, wg, wu, hbuf, wd, acc, d2d, tpl, tmi, rpl, rmi,
               send, recv, loc):
    tok_n = tok_hbm.shape[0]
    half_t = tok_n // 2
    ffn = wd_hbm.shape[1]
    half_f = ffn // 2
    n_chunk = len(cols)
    top_n = ids_ref.shape[1]
    opp = side // 2

    me = lax.axis_index("ep")
    core = lax.rem(me, CORES)
    xpos = lax.rem(me // CORES, side)
    ypos = me // (CORES * side)

    def dev(yy, xx, cc):
        return (lax.rem(yy, side) * side + lax.rem(xx, side)) * CORES + cc

    partner = dev(ypos, xpos, 1 - core)
    xp, xm, xo = dev(ypos, xpos + 1, core), dev(ypos, xpos + side - 1, core), dev(ypos, xpos + opp, core)
    yp, ym = dev(ypos + 1, xpos, core), dev(ypos + side - 1, xpos, core)

    barrier = pltpu.get_barrier_semaphore()
    for peer in (partner, xp, xm, xo, yp, ym):
        pl.semaphore_signal(barrier, inc=1, device_id={"ep": peer}, device_id_type=MESH)
    pl.semaphore_wait(barrier, 6)

    count = [0]
    sent = []

    def rcopy(src, dst, peer):
        i = count[0]
        count[0] += 1
        c = pltpu.make_async_remote_copy(src_ref=src, dst_ref=dst, send_sem=send.at[i], recv_sem=recv.at[i],
                                         device_id={"ep": peer}, device_id_type=MESH)
        sent.append(c)
        return c

    lcount = [0]

    def lcopy(src, dst):
        i = lcount[0]
        lcount[0] += 1
        c = pltpu.make_async_copy(src, dst, loc.at[i])
        c.start()
        return c

    tok_in = {0: rcopy(tok_hbm, xbuf.at[0, 1], partner), 3: rcopy(tok_hbm, xbuf.at[3, 0], xp),
              1: rcopy(tok_hbm, xbuf.at[1, 0], xm), 2: rcopy(tok_hbm, xbuf.at[2, 0], xo)}
    wgt_3 = rcopy(wg_hbm.at[0], wg.at[3], yp)
    wup_1 = rcopy(wu_hbm.at[0], wu.at[1], ym)
    wup_3 = rcopy(wu_hbm.at[0], wu.at[3], yp)
    wgt_1 = rcopy(wg_hbm.at[0], wg.at[1], ym)
    tok_in[0].start()
    wgt_3.start()
    wup_1.start()
    for r in (1, 3, 2):
        tok_in[r].start()
    wup_3.start()
    wgt_1.start()
    loc_x = lcopy(tok_hbm, xbuf.at[0, 0])
    loc_g = lcopy(wg_hbm.at[0], wg.at[0])
    loc_u = lcopy(wu_hbm.at[0], wu.at[0])
    loc_d = [lcopy(wd_hbm.at[0, :, pl.ds(c0, cw)], wd[k].at[0]) for k, (c0, cw) in enumerate(cols)]

    lane = lax.broadcasted_iota(jnp.int32, (tok_n, LANES), 1)
    picked = jnp.zeros((tok_n, LANES), F32)
    gates = jnp.zeros((tok_n, LANES), F32)
    for j in range(top_n):
        hit = ids_ref[:, j:j + 1] == lane
        picked = jnp.where(hit, 1.0, picked)
        gates = jnp.where(hit, gate_ref[:, j:j + 1], gates)
    earlier = lax.broadcasted_iota(jnp.int32, (tok_n, tok_n), 1) < lax.broadcasted_iota(jnp.int32, (tok_n, tok_n), 0)
    before = jnp.dot(jnp.where(earlier, 1.0, 0.0).astype(BF16), picked.astype(BF16), preferred_element_type=F32)
    gbuf[0, 0] = jnp.where(before < cnt_ref[0:1, :].astype(F32), gates, 0.0)

    def h_block(slot, r, c):
        x = xbuf[r, c]
        a = jnp.dot(x, wg[slot], preferred_element_type=F32)
        b = jnp.dot(x, wu[slot], preferred_element_type=F32)
        hbuf[slot, r, c] = (a * jax.nn.sigmoid(a) * b).astype(BF16)

    loc_x.wait()
    loc_g.wait()
    loc_u.wait()
    h_block(0, 0, 0)
    gate_in = {0: rcopy(gbuf.at[0, 0], gbuf.at[0, 1], partner), 3: rcopy(gbuf.at[0, 0], gbuf.at[3, 0], xp),
               1: rcopy(gbuf.at[0, 0], gbuf.at[1, 0], xm), 2: rcopy(gbuf.at[0, 0], gbuf.at[2, 0], xo)}
    for r in (0, 1, 3, 2):
        gate_in[r].start()
    tok_in[0].wait_recv()
    h_block(0, 0, 1)
    tok_fwd, gate_fwd = {}, {}
    for r in (1, 3, 2):
        tok_in[r].wait_recv()
        tok_fwd[r] = rcopy(xbuf.at[r, 0], xbuf.at[r, 1], partner)
        tok_fwd[r].start()
        h_block(0, r, 0)
    for r in (1, 3, 2):
        tok_fwd[r].wait_recv()
        h_block(0, r, 1)

    wgt_3.wait_recv()
    wgt_2 = rcopy(wg.at[3], wg.at[2], yp)
    wgt_2.start()
    wup_1.wait_recv()
    wup_2 = rcopy(wu.at[1], wu.at[2], ym)
    wup_2.start()

    own_p, own_m, fwd_p, fwd_m = [], [], [], []
    for k in range(n_chunk):
        loc_d[k].wait()
        own_p.append(rcopy(wd[k].at[0], wd[k].at[3], yp))
        own_m.append(rcopy(wd[k].at[0], wd[k].at[1], ym))
        fwd_p.append(rcopy(wd[k].at[3, pl.ds(0, half_f)], wd[k].at[2, pl.ds(0, half_f)], yp))
        fwd_m.append(rcopy(wd[k].at[1, pl.ds(half_f, half_f)], wd[k].at[2, pl.ds(half_f, half_f)], ym))
    for k in range(2):
        own_p[k].start()
        own_m[k].start()

    gate_in[0].wait_recv()
    for r in (1, 3, 2):
        gate_in[r].wait_recv()
        gate_fwd[r] = rcopy(gbuf.at[r, 0], gbuf.at[r, 1], partner)
        gate_fwd[r].start()

    def h_all(slot):
        def body(i, _):
            h_block(slot, i // CORES, lax.rem(i, CORES))
            return 0
        lax.fori_loop(0, side * CORES, body, 0)

    for r in (1, 3, 2):
        gate_fwd[r].wait_recv()

    def sel_body(i, _):
        g = gbuf[i // CORES, lax.rem(i, CORES)]
        for s in range(side):
            one = jnp.sum(jnp.where(lane == dev(ypos + s, xpos, core), g, 0.0), axis=1, keepdims=True)
            gsel[s, i // CORES, lax.rem(i, CORES)] = jnp.broadcast_to(one, (tok_n, LANES))
        return 0
    lax.fori_loop(0, side * CORES, sel_body, 0)

    wup_3.wait_recv()
    h_all(3)
    wgt_1.wait_recv()
    h_all(1)
    wgt_2.wait_recv()
    wup_2.wait_recv()
    h_all(2)

    def gated(s, r, c, k):
        y = jnp.dot(hbuf[s, r, c], wd[k][s], preferred_element_type=F32).astype(BF16).astype(F32)
        g = gsel[s, r, c]
        return jnp.concatenate([jnp.where(g > 0.0, g * y[:, q:q + LANES], 0.0) for q in range(0, cols[k][1], LANES)], axis=1)

    exch, t_p, t_m, r_p, r_m = [], [], [], [], []

    def stage_a(k):
        own_p[k].wait_recv()
        fwd_p[k].start()
        own_m[k].wait_recv()
        fwd_m[k].start()
        if k + 2 < n_chunk:
            own_p[k + 2].start()
            own_m[k + 2].start()

        def first(i, _):
            r, c = i // CORES, lax.rem(i, CORES)
            acc[k][c, r] = gated(0, r, c, k) + gated(1, r, c, k) + gated(3, r, c, k)
            return 0
        lax.fori_loop(0, side * CORES, first, 0)
        fwd_p[k].wait_recv()
        fwd_m[k].wait_recv()

        def last(i, _):
            r, c = lax.rem(i, side), 1 - i // side
            acc[k][c, r] = acc[k][c, r] + gated(2, r, c, k)
            return 0
        lax.fori_loop(0, side, last, 0)
        exch.append(rcopy(acc[k].at[1], d2d[k], partner))
        exch[k].start()
        lax.fori_loop(side, side * CORES, last, 0)

    def stage_b(k):
        exch[k].wait_recv()
        acc[k][0, 2] = acc[k][0, 2] + d2d[k][2]
        t_p.append(rcopy(acc[k].at[0, 2, pl.ds(0, half_t)], tpl[k], xp))
        t_m.append(rcopy(acc[k].at[0, 2, pl.ds(half_t, half_t)], tmi[k], xm))
        t_p[k].start()
        t_m[k].start()
        for r in (1, 3, 0):
            acc[k][0, r] = acc[k][0, r] + d2d[k][r]

    def stage_c(k):
        t_p[k].wait_recv()
        acc[k][0, 1, pl.ds(0, half_t)] = acc[k][0, 1, pl.ds(0, half_t)] + tpl[k][...]
        r_p.append(rcopy(acc[k].at[0, 1], rpl[k], xp))
        r_p[k].start()
        t_m[k].wait_recv()
        acc[k][0, 3, pl.ds(half_t, half_t)] = acc[k][0, 3, pl.ds(half_t, half_t)] + tmi[k][...]
        r_m.append(rcopy(acc[k].at[0, 3], rmi[k], xm))
        r_m[k].start()

    def stage_d(k):
        r_p[k].wait_recv()
        r_m[k].wait_recv()
        c0, cw = cols[k]
        total = xbuf[0, 0, :, c0:c0 + cw].astype(F32) + acc[k][0, 0]
        out_ref[:, c0:c0 + cw] = (total + rpl[k][...] + rmi[k][...]).astype(BF16)

    for k in range(n_chunk):
        stage_a(k)
        stage_b(k)
        if k >= 1:
            stage_c(k - 1)
        if k >= 2:
            stage_d(k - 2)
    stage_c(n_chunk - 1)
    if n_chunk >= 2:
        stage_d(n_chunk - 2)
    stage_d(n_chunk - 1)
    for c in sent:
        c.wait_send()


def solution(mesh):
    group_size = mesh.shape["ep"]
    side = math.isqrt(group_size // CORES)
    row_spec = P(("dp", "ep"))

    def local_step(tokens, expert_ids, gate_w, route_counts, w_gate, w_up, w_down):
        tok_n, dim = tokens.shape
        ffn = w_gate.shape[2]
        widths = CHUNKS if sum(CHUNKS) == dim else (LANES,) * (dim // LANES)
        cols = tuple((sum(widths[:k]), cw) for k, cw in enumerate(widths))
        counts = jnp.pad(route_counts, ((0, 0), (0, LANES - route_counts.shape[1])))
        n_copy = 4 + 4 + 4 + 3 + 3 + 2 + 9 * len(cols)
        vmem = pl.BlockSpec(memory_space=pltpu.VMEM)
        anym = pl.BlockSpec(memory_space=pl.ANY)
        return pl.pallas_call(
            lambda *refs: call_kernel(side, cols, refs),
            out_shape=jax.ShapeDtypeStruct((tok_n, dim), BF16),
            in_specs=[vmem] * 3 + [anym] * 4,
            out_specs=vmem,
            scratch_shapes=[
                pltpu.VMEM((side, CORES, tok_n, dim), BF16),
                pltpu.VMEM((side, CORES, tok_n, LANES), F32),
                pltpu.VMEM((side, side, CORES, tok_n, LANES), F32),
                pltpu.VMEM((side, dim, ffn), BF16),
                pltpu.VMEM((side, dim, ffn), BF16),
                pltpu.VMEM((side, side, CORES, tok_n, ffn), BF16),
                [pltpu.VMEM((side, ffn, cw), BF16) for _, cw in cols],
                [pltpu.VMEM((CORES, side, tok_n, cw), F32) for _, cw in cols],
                [pltpu.VMEM((side, tok_n, cw), F32) for _, cw in cols],
                [pltpu.VMEM((tok_n // 2, cw), F32) for _, cw in cols],
                [pltpu.VMEM((tok_n // 2, cw), F32) for _, cw in cols],
                [pltpu.VMEM((tok_n, cw), F32) for _, cw in cols],
                [pltpu.VMEM((tok_n, cw), F32) for _, cw in cols],
                pltpu.SemaphoreType.DMA((n_copy,)),
                pltpu.SemaphoreType.DMA((n_copy,)),
                pltpu.SemaphoreType.DMA((3 + len(cols),)),
            ],
            compiler_params=pltpu.CompilerParams(collective_id=0, has_side_effects=True, vmem_limit_bytes=60 * 2 ** 20),
            name="moe_kernel",
        )(expert_ids, gate_w, counts, tokens, w_gate, w_up, w_down)

    def call_kernel(side, cols, refs):
        moe_kernel(side, cols, *refs)

    return jax.shard_map(local_step, mesh=mesh, in_specs=(row_spec, row_spec, row_spec, row_spec, P("ep"), P("ep"), P("ep")), out_specs=row_spec, check_vma=False)
```

time: 454 us -> 146 us (0.32)
  the two profiles are of different devices: /device:TPU:103 before, /device:TPU:97 now
where the time goes in v1:
time: 146 us
  Pallas kernels  141 us (97%)
  local copies, waits for them, and re-layouts  5.38 us (4%)
    pallas_call x1, Pallas kernels, local_step(): pl.pallas_call(lambda *refs: call_kernel(side, cols, refs), out_shape=jax...  141 us
    unnamed x5, local copies, waits for them, and re-layouts  4.16 us

profile of v1, /device:TPU:97, one launch (start us, length us, event | category | flops | bytes accessed | tf_op | source)
XLA Modules:
  0.0 146.2 jit_solution(3859691196886922118)
XLA Ops:
  0.0 1.2 pad.4.refs_2_
  1.2 0.0 copy-start
  1.2 1.5 %copy.8.refs_0_ = s32[256,8]{1,0:T(8,128)} copy(s32[256,8]{0,1:T(8,128)} %param.8) | data formatting | bytes 16384 | tf_op args[1]
  2.7 0.0 copy-done
  2.7 0.8 copy.9.refs_1_
  3.5 140.8 %moe_kernel.1 = bf16[256,1024]{1,0:T(8,128)(2,1)} custom-call(s32[256,8]{1,0:T(8,128)} %copy.8.refs_0_, f32[256,8]{1,0:T(8,128)} %copy.9.refs_1_, s32[1,128]{1,0:T(1,128)} %pad.4.refs_2_, bf16[256,1024]{1,0:T(8,128)(2,1)} %refs_3_.1, bf16[1,1024,512]{2,1,0:T(8,128)(2,1)} %refs_4_.1, bf16[1,1024,512]{2,1,0:T(8,128)(2,1)} %refs_5_.1, bf16[1,512,1024]{2,1,0:T(8,128)(2,1)} %refs_6_.1), custom_call_target="tpu_custom_call" | custom-call | tf_op jit(solution)/shard_map/moe_kernel/pallas_call | solution.py:259
  144.3 1.9 %copy.11 = bf16[256,1024]{1,0:T(8,128)(2,1)} copy(bf16[256,1024]{1,0:T(8,128)(2,1)} %moe_kernel.1) | data formatting | bytes 1048576
Async XLA Ops:
  1.2 1.5 %copy-start = (f32[256,8]{0,1:T(8,128)S(1)}, f32[256,8]{0,1:T(8,128)}, u32[]{:S(2)}) copy-start(f32[256,8]{0,1:T(8,128)} %param.9) | copy-start | bytes 24580

commit v2 on v1

v2 whole, which is shorter than its diff:
```python
import math

import jax
import jax.numpy as jnp
from jax import lax
from jax.experimental import pallas as pl
from jax.experimental.pallas import tpu as pltpu
from jax.sharding import PartitionSpec as P

MESH = pl.DeviceIdType.MESH
CORES = 2
LANES = 128
CHUNKS = (128,) * 8
AHEAD = 2
PIECES = 2
F32 = jnp.float32
BF16 = jnp.bfloat16


def moe_kernel(side, cols, ids_ref, gate_ref, cnt_ref, tok_hbm, wg_hbm, wu_hbm, wd_hbm, out_ref,
               xbuf, gbuf, gsel, wg, wu, hbuf, wd, acc, d2d, tpl, tmi, rpl, rmi,
               send, recv, loc):
    tok_n = tok_hbm.shape[0]
    half_t = tok_n // 2
    ffn = wd_hbm.shape[1]
    half_f = ffn // 2
    n_chunk = len(cols)
    top_n = ids_ref.shape[0]
    opp = side // 2

    me = lax.axis_index("ep")
    core = lax.rem(me, CORES)
    xpos = lax.rem(me // CORES, side)
    ypos = me // (CORES * side)

    def dev(yy, xx, cc):
        return (lax.rem(yy, side) * side + lax.rem(xx, side)) * CORES + cc

    partner = dev(ypos, xpos, 1 - core)
    xp, xm, xo = dev(ypos, xpos + 1, core), dev(ypos, xpos + side - 1, core), dev(ypos, xpos + opp, core)
    yp, ym = dev(ypos + 1, xpos, core), dev(ypos + side - 1, xpos, core)

    barrier = pltpu.get_barrier_semaphore()
    for peer in (partner, xp, xm, xo, yp, ym):
        pl.semaphore_signal(barrier, inc=1, device_id={"ep": peer}, device_id_type=MESH)
    pl.semaphore_wait(barrier, 6)

    count = [0]
    sent = []

    def rcopy(src, dst, peer):
        i = count[0]
        count[0] += 1
        c = pltpu.make_async_remote_copy(src_ref=src, dst_ref=dst, send_sem=send.at[i], recv_sem=recv.at[i],
                                         device_id={"ep": peer}, device_id_type=MESH)
        sent.append(c)
        return c

    lcount = [0]

    def lcopy(src, dst):
        i = lcount[0]
        lcount[0] += 1
        c = pltpu.make_async_copy(src, dst, loc.at[i])
        c.start()
        return c

    tok_in = {0: rcopy(tok_hbm, xbuf.at[0, 1], partner), 3: rcopy(tok_hbm, xbuf.at[3, 0], xp),
              1: rcopy(tok_hbm, xbuf.at[1, 0], xm)}
    wgt_3 = rcopy(wg_hbm.at[0], wg.at[3], yp)
    wup_1 = rcopy(wu_hbm.at[0], wu.at[1], ym)
    wup_3 = rcopy(wu_hbm.at[0], wu.at[3], yp)
    wgt_1 = rcopy(wg_hbm.at[0], wg.at[1], ym)
    tok_in[0].start()
    wgt_3.start()
    wup_1.start()
    for r in (1, 3):
        tok_in[r].start()
    wup_3.start()
    wgt_1.start()
    loc_x = lcopy(tok_hbm, xbuf.at[0, 0])
    loc_g = lcopy(wg_hbm.at[0], wg.at[0])
    loc_u = lcopy(wu_hbm.at[0], wu.at[0])
    loc_d = [lcopy(wd_hbm.at[0, :, pl.ds(c0, cw)], wd[k].at[0]) for k, (c0, cw) in enumerate(cols)]

    own_p, own_m, fwd_p, fwd_m = [], [], [], []
    for k in range(n_chunk):
        own_p.append(rcopy(wd[k].at[0], wd[k].at[3], yp))
        own_m.append(rcopy(wd[k].at[0], wd[k].at[1], ym))
        fwd_p.append(rcopy(wd[k].at[3, pl.ds(0, half_f)], wd[k].at[2, pl.ds(0, half_f)], yp))
        fwd_m.append(rcopy(wd[k].at[1, pl.ds(half_f, half_f)], wd[k].at[2, pl.ds(half_f, half_f)], ym))
    for k in range(n_chunk):
        loc_d[k].wait()
    for k in range(min(AHEAD, n_chunk)):
        own_p[k].start()
        own_m[k].start()

    n_exp = cnt_ref.shape[1]
    row = lax.broadcasted_iota(jnp.int32, (n_exp, tok_n), 0)
    picked = jnp.zeros((n_exp, tok_n), F32)
    gates = jnp.zeros((n_exp, tok_n), F32)
    for j in range(top_n):
        hit = ids_ref[j:j + 1, :] == row
        picked = jnp.where(hit, 1.0, picked)
        gates = jnp.where(hit, gate_ref[j:j + 1, :], gates)
    earlier = lax.broadcasted_iota(jnp.int32, (tok_n, tok_n), 0) < lax.broadcasted_iota(jnp.int32, (tok_n, tok_n), 1)
    before = jnp.dot(picked.astype(BF16), jnp.where(earlier, 1.0, 0.0).astype(BF16), preferred_element_type=F32)
    limit = jnp.transpose(jnp.broadcast_to(cnt_ref[0:1, :].astype(F32), (8, n_exp)))[:, 0:1]
    gbuf[0, 0] = jnp.where(before < limit, gates, 0.0)

    def h_block(slot, r, c):
        x = xbuf[r, c]
        a = jnp.dot(x, wg[slot], preferred_element_type=F32)
        b = jnp.dot(x, wu[slot], preferred_element_type=F32)
        hbuf[slot, r, c] = (a * jax.nn.sigmoid(a) * b).astype(BF16)

    loc_x.wait()
    loc_g.wait()
    loc_u.wait()
    h_block(0, 0, 0)
    gate_in = {0: rcopy(gbuf.at[0, 0], gbuf.at[0, 1], partner), 3: rcopy(gbuf.at[0, 0], gbuf.at[3, 0], xp),
               1: rcopy(gbuf.at[0, 0], gbuf.at[1, 0], xm), 2: rcopy(gbuf.at[0, 0], gbuf.at[2, 0], xo)}
    for r in (0, 1, 3, 2):
        gate_in[r].start()
    tok_in[0].wait_recv()
    h_block(0, 0, 1)
    tok_fwd, gate_fwd = {}, {}
    lo_t, hi_t = pl.ds(0, half_t), pl.ds(half_t, half_t)
    tok_in[3].wait_recv()
    tok_fwd[3] = rcopy(xbuf.at[3, 0], xbuf.at[3, 1], partner)
    tok_2p = rcopy(xbuf.at[3, 0, lo_t], xbuf.at[2, 0, lo_t], xp)
    tok_2p.start()
    tok_fwd[3].start()
    tok_in[1].wait_recv()
    tok_fwd[1] = rcopy(xbuf.at[1, 0], xbuf.at[1, 1], partner)
    tok_2m = rcopy(xbuf.at[1, 0, hi_t], xbuf.at[2, 0, hi_t], xm)
    tok_2m.start()
    tok_fwd[1].start()
    h_block(0, 3, 0)
    h_block(0, 1, 0)
    tok_fwd[3].wait_recv()
    h_block(0, 3, 1)
    tok_fwd[1].wait_recv()
    h_block(0, 1, 1)
    tok_2p.wait_recv()
    tok_2m.wait_recv()
    tok_fwd[2] = rcopy(xbuf.at[2, 0], xbuf.at[2, 1], partner)
    tok_fwd[2].start()
    h_block(0, 2, 0)
    tok_fwd[2].wait_recv()
    h_block(0, 2, 1)

    pieces = [pl.ds(q * ffn // PIECES, ffn // PIECES) for q in range(PIECES)]
    wgt_3.wait_recv()
    wgt_2 = [rcopy(wg.at[3, :, q], wg.at[2, :, q], yp) for q in pieces]
    for w in wgt_2:
        w.start()
    wup_1.wait_recv()
    wup_2 = [rcopy(wu.at[1, :, q], wu.at[2, :, q], ym) for q in pieces]
    for w in wup_2:
        w.start()

    gate_in[0].wait_recv()
    for r in (1, 3, 2):
        gate_in[r].wait_recv()
        gate_fwd[r] = rcopy(gbuf.at[r, 0], gbuf.at[r, 1], partner)
        gate_fwd[r].start()

    def h_all(slot, q):
        def body(r, _):
            x = xbuf[r].reshape(CORES * tok_n, xbuf.shape[3])
            a = jnp.dot(x, wg[slot, :, q], preferred_element_type=F32)
            b = jnp.dot(x, wu[slot, :, q], preferred_element_type=F32)
            hbuf[slot, r, :, :, q] = (a * jax.nn.sigmoid(a) * b).astype(BF16).reshape(CORES, tok_n, a.shape[1])
            return 0
        lax.fori_loop(0, side, body, 0)

    for r in (1, 3, 2):
        gate_fwd[r].wait_recv()

    lane = lax.broadcasted_iota(jnp.int32, (tok_n, n_exp), 1)

    def sel_body(i, _):
        g = jnp.transpose(gbuf[i // CORES, lax.rem(i, CORES)])
        for s in range(side):
            one = jnp.sum(jnp.where(lane == dev(ypos + s, xpos, core), g, 0.0), axis=1, keepdims=True)
            gsel[s, i // CORES, lax.rem(i, CORES)] = jnp.broadcast_to(one, (tok_n, LANES))
        return 0
    lax.fori_loop(0, side * CORES, sel_body, 0)

    wup_3.wait_recv()
    h_all(3, pl.ds(0, ffn))
    wgt_1.wait_recv()
    h_all(1, pl.ds(0, ffn))

    def gated(s, r, k):
        y = jnp.dot(hbuf[s, r].reshape(CORES * tok_n, ffn), wd[k][s], preferred_element_type=F32).astype(BF16).astype(F32)
        g = gsel[s, r].reshape(CORES * tok_n, LANES)
        z = [jnp.where(g > 0.0, g * y[:, q:q + LANES], 0.0) for q in range(0, cols[k][1], LANES)]
        return jnp.concatenate(z, axis=1).reshape(CORES, tok_n, cols[k][1])

    far, t_p, t_m, r_p, r_m, near = [], [], [], [], [], []

    def place(i):
        return jnp.where(i == 0, 2, jnp.where(i == 1, 1, jnp.where(i == 2, 3, 0)))

    def forward(k):
        own_p[k].wait_recv()
        fwd_p[k].start()
        own_m[k].wait_recv()
        fwd_m[k].start()
        if k + AHEAD < n_chunk:
            own_p[k + AHEAD].start()
            own_m[k + AHEAD].start()

    def first(k):
        def body(i, _):
            r = place(i)
            acc[k][:, i] = gated(0, r, k) + gated(1, r, k) + gated(3, r, k)
            return 0
        lax.fori_loop(0, side, body, 0)

    def last(k):
        fwd_p[k].wait_recv()
        fwd_m[k].wait_recv()
        acc[k][:, 0] = acc[k][:, 0] + gated(2, 2, k)
        far.append(rcopy(acc[k].at[1, pl.ds(0, 1)], d2d[k].at[pl.ds(0, 1)], partner))
        far[k].start()
        for i, r in ((1, 1), (2, 3), (3, 0)):
            acc[k][:, i] = acc[k][:, i] + gated(2, r, k)
        near.append(rcopy(acc[k].at[1, pl.ds(1, side - 1)], d2d[k].at[pl.ds(1, side - 1)], partner))
        near[k].start()

    def stage_b(k):
        far[k].wait_recv()
        acc[k][0, 0] = acc[k][0, 0] + d2d[k][0]
        t_p.append(rcopy(acc[k].at[0, 0, lo_t], tpl[k], xp))
        t_m.append(rcopy(acc[k].at[0, 0, hi_t], tmi[k], xm))
        t_p[k].start()
        t_m[k].start()
        near[k].wait_recv()
        for i in range(1, side):
            acc[k][0, i] = acc[k][0, i] + d2d[k][i]

    def stage_c(k):
        t_p[k].wait_recv()
        acc[k][0, 1, lo_t] = acc[k][0, 1, lo_t] + tpl[k][...]
        r_p.append(rcopy(acc[k].at[0, 1], rpl[k], xp))
        r_p[k].start()
        t_m[k].wait_recv()
        acc[k][0, 2, hi_t] = acc[k][0, 2, hi_t] + tmi[k][...]
        r_m.append(rcopy(acc[k].at[0, 2], rmi[k], xm))
        r_m[k].start()

    def stage_d(k):
        r_p[k].wait_recv()
        r_m[k].wait_recv()
        c0, cw = cols[k]
        total = xbuf[0, 0, :, c0:c0 + cw].astype(F32) + acc[k][0, 3]
        out_ref[:, c0:c0 + cw] = (total + rpl[k][...] + rmi[k][...]).astype(BF16)

    for k in range(min(2, n_chunk)):
        forward(k)
    first(0)
    for p, q in enumerate(pieces):
        wgt_2[p].wait_recv()
        wup_2[p].wait_recv()
        h_all(2, q)
        if p == 0 and n_chunk > 1:
            first(1)
    for k in range(n_chunk):
        last(k)
        if k >= 1 and k + 1 < n_chunk:
            first(k + 1)
        stage_b(k)
        if k >= 1:
            stage_c(k - 1)
        if k + 2 < n_chunk:
            forward(k + 2)
        if k >= 2:
            stage_d(k - 2)
    stage_c(n_chunk - 1)
    for k in range(max(n_chunk - 2, 0), n_chunk):
        stage_d(k)
    for c in sent:
        c.wait_send()


def solution(mesh):
    group_size = mesh.shape["ep"]
    side = math.isqrt(group_size // CORES)
    row_spec = P(("dp", "ep"))

    def local_step(tokens, expert_ids, gate_w, route_counts, w_gate, w_up, w_down):
        tok_n, dim = tokens.shape
        ffn = w_gate.shape[2]
        n_exp = route_counts.shape[1]
        widths = CHUNKS if sum(CHUNKS) == dim else (LANES,) * (dim // LANES)
        cols = tuple((sum(widths[:k]), cw) for k, cw in enumerate(widths))
        n_copy = 5 + 4 + 4 + 3 + 3 + 2 * PIECES + 10 * len(cols)
        vmem = pl.BlockSpec(memory_space=pltpu.VMEM)
        anym = pl.BlockSpec(memory_space=pl.ANY)
        return pl.pallas_call(
            lambda *refs: call_kernel(side, cols, refs),
            out_shape=jax.ShapeDtypeStruct((tok_n, dim), BF16),
            in_specs=[vmem] * 3 + [anym] * 4,
            out_specs=vmem,
            scratch_shapes=[
                pltpu.VMEM((side, CORES, tok_n, dim), BF16),
                pltpu.VMEM((side, CORES, n_exp, tok_n), F32),
                pltpu.VMEM((side, side, CORES, tok_n, LANES), F32),
                pltpu.VMEM((side, dim, ffn), BF16),
                pltpu.VMEM((side, dim, ffn), BF16),
                pltpu.VMEM((side, side, CORES, tok_n, ffn), BF16),
                [pltpu.VMEM((side, ffn, cw), BF16) for _, cw in cols],
                [pltpu.VMEM((CORES, side, tok_n, cw), F32) for _, cw in cols],
                [pltpu.VMEM((side, tok_n, cw), F32) for _, cw in cols],
                [pltpu.VMEM((tok_n // 2, cw), F32) for _, cw in cols],
                [pltpu.VMEM((tok_n // 2, cw), F32) for _, cw in cols],
                [pltpu.VMEM((tok_n, cw), F32) for _, cw in cols],
                [pltpu.VMEM((tok_n, cw), F32) for _, cw in cols],
                pltpu.SemaphoreType.DMA((n_copy,)),
                pltpu.SemaphoreType.DMA((n_copy,)),
                pltpu.SemaphoreType.DMA((3 + len(cols),)),
            ],
            compiler_params=pltpu.CompilerParams(collective_id=0, has_side_effects=True, vmem_limit_bytes=60 * 2 ** 20),
            name="moe_kernel",
        )(expert_ids.T, gate_w.T, route_counts, tokens, w_gate, w_up, w_down)

    def call_kernel(side, cols, refs):
        moe_kernel(side, cols, *refs)

    return jax.shard_map(local_step, mesh=mesh, in_specs=(row_spec, row_spec, row_spec, row_spec, P("ep"), P("ep"), P("ep")), out_specs=row_spec, check_vma=False)
```

time: 146 us -> 136 us (0.932)
  Pallas kernels: 141 us -> 134 us
  local copies, waits for them, and re-layouts: 5.38 us -> 1.87 us
    pallas_call x1, Pallas kernels: 141 us -> 134 us  [local_step(): pl.pallas_call(lambda *refs: call_kernel(side, cols, refs), out_shape=jax...]
    unnamed x5 -> x1, local copies, waits for them, and re-layouts: 4.16 us -> 1.87 us
where the time goes in v2:
time: 136 us
  Pallas kernels  134 us (99%)
  local copies, waits for them, and re-layouts  1.87 us (1%)
    pallas_call x1, Pallas kernels, local_step(): pl.pallas_call(lambda *refs: call_kernel(side, cols, refs), out_shape=jax...  134 us

profile of v2, /device:TPU:97, one launch (start us, length us, event | category | flops | bytes accessed | tf_op | source)
XLA Modules:
  0.0 135.5 jit_solution(6068041678014547458)
XLA Ops:
  0.0 133.6 %moe_kernel.1 = bf16[256,1024]{1,0:T(8,128)(2,1)} custom-call(s32[8,256]{1,0:T(8,128)} %bitcast.2, f32[8,256]{1,0:T(8,128)} %bitcast.3, s32[1,32]{1,0:T(1,128)} %refs_2_.1, bf16[256,1024]{1,0:T(8,128)(2,1)} %refs_3_.1, bf16[1,1024,512]{2,1,0:T(8,128)(2,1)} %refs_4_.1, bf16[1,1024,512]{2,1,0:T(8,128)(2,1)} %refs_5_.1, bf16[1,512,1024]{2,1,0:T(8,128)(2,1)} %refs_6_.1), custom_call_target="tpu_custom_call" | custom-call | tf_op jit(solution)/shard_map/moe_kernel/pallas_call | solution.py:303
  133.6 1.9 %copy.9 = bf16[256,1024]{1,0:T(8,128)(2,1)} copy(bf16[256,1024]{1,0:T(8,128)(2,1)} %moe_kernel.1) | data formatting | bytes 1048576

commit v3 on v2

--- a/solution.py
+++ b/solution.py
@@ -11,8 +11,8 @@
 CORES = 2
 LANES = 128
 CHUNKS = (128,) * 8
-AHEAD = 2
 PIECES = 2
+MID = 1
 F32 = jnp.float32
 BF16 = jnp.bfloat16
 
@@ -83,17 +83,27 @@
     loc_u = lcopy(wu_hbm.at[0], wu.at[0])
     loc_d = [lcopy(wd_hbm.at[0, :, pl.ds(c0, cw)], wd[k].at[0]) for k, (c0, cw) in enumerate(cols)]
 
-    own_p, own_m, fwd_p, fwd_m = [], [], [], []
+    lo_f, hi_f = pl.ds(0, half_f), pl.ds(half_f, half_f)
+    lead, rest, hop = [], [], []
     for k in range(n_chunk):
-        own_p.append(rcopy(wd[k].at[0], wd[k].at[3], yp))
-        own_m.append(rcopy(wd[k].at[0], wd[k].at[1], ym))
-        fwd_p.append(rcopy(wd[k].at[3, pl.ds(0, half_f)], wd[k].at[2, pl.ds(0, half_f)], yp))
-        fwd_m.append(rcopy(wd[k].at[1, pl.ds(half_f, half_f)], wd[k].at[2, pl.ds(half_f, half_f)], ym))
+        lead.append((rcopy(wd[k].at[0, lo_f], wd[k].at[3, lo_f], yp), rcopy(wd[k].at[0, hi_f], wd[k].at[1, hi_f], ym)))
+        rest.append((rcopy(wd[k].at[0, hi_f], wd[k].at[3, hi_f], yp), rcopy(wd[k].at[0, lo_f], wd[k].at[1, lo_f], ym)))
+        hop.append((rcopy(wd[k].at[3, lo_f], wd[k].at[2, lo_f], yp), rcopy(wd[k].at[1, hi_f], wd[k].at[2, hi_f], ym)))
+
+    def start(copies):
+        for c in copies:
+            c.start()
+
+    def arrive(copies):
+        for c in copies:
+            c.wait_recv()
+
     for k in range(n_chunk):
         loc_d[k].wait()
-    for k in range(min(AHEAD, n_chunk)):
-        own_p[k].start()
-        own_m[k].start()
+    start(lead[0])
+    start(rest[0])
+    if n_chunk > 1:
+        start(lead[1])
 
     n_exp = cnt_ref.shape[1]
     row = lax.broadcasted_iota(jnp.int32, (n_exp, tok_n), 0)
@@ -166,12 +176,15 @@
         gate_fwd[r] = rcopy(gbuf.at[r, 0], gbuf.at[r, 1], partner)
         gate_fwd[r].start()
 
+    def h_row(slot, r, q):
+        x = xbuf[r].reshape(CORES * tok_n, xbuf.shape[3])
+        a = jnp.dot(x, wg[slot, :, q], preferred_element_type=F32)
+        b = jnp.dot(x, wu[slot, :, q], preferred_element_type=F32)
+        hbuf[slot, r, :, :, q] = (a * jax.nn.sigmoid(a) * b).astype(BF16).reshape(CORES, tok_n, a.shape[1])
+
     def h_all(slot, q):
         def body(r, _):
-            x = xbuf[r].reshape(CORES * tok_n, xbuf.shape[3])
-            a = jnp.dot(x, wg[slot, :, q], preferred_element_type=F32)
-            b = jnp.dot(x, wu[slot, :, q], preferred_element_type=F32)
-            hbuf[slot, r, :, :, q] = (a * jax.nn.sigmoid(a) * b).astype(BF16).reshape(CORES, tok_n, a.shape[1])
+            h_row(slot, r, q)
             return 0
         lax.fori_loop(0, side, body, 0)
 
@@ -205,39 +218,42 @@
         return jnp.where(i == 0, 2, jnp.where(i == 1, 1, jnp.where(i == 2, 3, 0)))
 
     def forward(k):
-        own_p[k].wait_recv()
-        fwd_p[k].start()
-        own_m[k].wait_recv()
-        fwd_m[k].start()
-        if k + AHEAD < n_chunk:
-            own_p[k + AHEAD].start()
-            own_m[k + AHEAD].start()
-
-    def first(k):
+        for c, f in zip(lead[k], hop[k]):
+            c.wait_recv()
+            f.start()
+        if k + 1 < n_chunk:
+            start(rest[k + 1])
+        if k + 2 < n_chunk:
+            start(lead[k + 2])
+
+    def first(k, begin, end):
+        if begin == 0:
+            arrive(rest[k])
+
         def body(i, _):
             r = place(i)
             acc[k][:, i] = gated(0, r, k) + gated(1, r, k) + gated(3, r, k)
             return 0
-        lax.fori_loop(0, side, body, 0)
-
-    def last(k):
-        fwd_p[k].wait_recv()
-        fwd_m[k].wait_recv()
-        acc[k][:, 0] = acc[k][:, 0] + gated(2, 2, k)
-        far.append(rcopy(acc[k].at[1, pl.ds(0, 1)], d2d[k].at[pl.ds(0, 1)], partner))
-        far[k].start()
-        for i, r in ((1, 1), (2, 3), (3, 0)):
-            acc[k][:, i] = acc[k][:, i] + gated(2, r, k)
-        near.append(rcopy(acc[k].at[1, pl.ds(1, side - 1)], d2d[k].at[pl.ds(1, side - 1)], partner))
-        near[k].start()
-
-    def stage_b(k):
+        lax.fori_loop(begin, end, body, 0)
+
+    def add_two_hop(k, i, r):
+        acc[k][:, i] = acc[k][:, i] + gated(2, r, k)
+        if i == 0:
+            far.append(rcopy(acc[k].at[1, pl.ds(0, 1)], d2d[k].at[pl.ds(0, 1)], partner))
+            far[k].start()
+        if i == side - 1:
+            near.append(rcopy(acc[k].at[1, pl.ds(1, side - 1)], d2d[k].at[pl.ds(1, side - 1)], partner))
+            near[k].start()
+
+    def stage_far(k):
         far[k].wait_recv()
         acc[k][0, 0] = acc[k][0, 0] + d2d[k][0]
         t_p.append(rcopy(acc[k].at[0, 0, lo_t], tpl[k], xp))
         t_m.append(rcopy(acc[k].at[0, 0, hi_t], tmi[k], xm))
         t_p[k].start()
         t_m[k].start()
+
+    def stage_near(k):
         near[k].wait_recv()
         for i in range(1, side):
             acc[k][0, i] = acc[k][0, i] + d2d[k][i]
@@ -259,24 +275,41 @@
         total = xbuf[0, 0, :, c0:c0 + cw].astype(F32) + acc[k][0, 3]
         out_ref[:, c0:c0 + cw] = (total + rpl[k][...] + rmi[k][...]).astype(BF16)
 
+    blocks = ((0, 2), (1, 1), (2, 3), (3, 0))
     for k in range(min(2, n_chunk)):
         forward(k)
-    first(0)
-    for p, q in enumerate(pieces):
+    first(0, 0, side)
+    for p, q in enumerate(pieces[:-1]):
         wgt_2[p].wait_recv()
         wup_2[p].wait_recv()
         h_all(2, q)
-        if p == 0 and n_chunk > 1:
-            first(1)
+    wgt_2[-1].wait_recv()
+    wup_2[-1].wait_recv()
+    for i, r in blocks:
+        h_row(2, r, pieces[-1])
+        if i == 0:
+            arrive(hop[0])
+        add_two_hop(0, i, r)
+        if i == 2:
+            stage_far(0)
     for k in range(n_chunk):
-        last(k)
-        if k >= 1 and k + 1 < n_chunk:
-            first(k + 1)
-        stage_b(k)
-        if k >= 1:
+        if k > 0:
+            arrive(hop[k])
+            for i, r in blocks:
+                add_two_hop(k, i, r)
+        if k + 1 < n_chunk:
+            first(k + 1, 0, MID)
+        if k > 0:
+            stage_far(k)
+        if k > 1:
             stage_c(k - 1)
         if k + 2 < n_chunk:
             forward(k + 2)
+        if k + 1 < n_chunk:
+            first(k + 1, MID, side)
+        stage_near(k)
+        if k == 0 and n_chunk > 1:
+            stage_c(0)
         if k >= 2:
             stage_d(k - 2)
     stage_c(n_chunk - 1)
@@ -297,12 +330,12 @@
         n_exp = route_counts.shape[1]
         widths = CHUNKS if sum(CHUNKS) == dim else (LANES,) * (dim // LANES)
         cols = tuple((sum(widths[:k]), cw) for k, cw in enumerate(widths))
-        n_copy = 5 + 4 + 4 + 3 + 3 + 2 * PIECES + 10 * len(cols)
+        n_copy = 5 + 4 + 4 + 3 + 3 + 2 * PIECES + 12 * len(cols)
         vmem = pl.BlockSpec(memory_space=pltpu.VMEM)
         anym = pl.BlockSpec(memory_space=pl.ANY)
         return pl.pallas_call(
             lambda *refs: call_kernel(side, cols, refs),
-            out_shape=jax.ShapeDtypeStruct((tok_n, dim), BF16),
+            out_shape=pltpu.VMEM((tok_n, dim), BF16),
             in_specs=[vmem] * 3 + [anym] * 4,
             out_specs=vmem,
             scratch_shapes=[

time: 136 us -> 130 us (0.956)
  Pallas kernels: 134 us -> 129 us
    pallas_call x1, Pallas kernels: 134 us -> 129 us  [local_step(): pl.pallas_call(lambda *refs: call_kernel(side, cols, refs), out_shape=plt...]
where the time goes in v3:
time: 130 us
  Pallas kernels  129 us (99%)
    pallas_call x1, Pallas kernels, local_step(): pl.pallas_call(lambda *refs: call_kernel(side, cols, refs), out_shape=plt...  129 us

profile of v3, /device:TPU:97, one launch (start us, length us, event | category | flops | bytes accessed | tf_op | source)
XLA Modules:
  0.0 129.9 jit_solution(13564837625502388791)
XLA Ops:
  0.0 129.1 %moe_kernel.1 = bf16[256,1024]{1,0:T(8,128)(2,1)S(1)} custom-call(s32[8,256]{1,0:T(8,128)} %bitcast.2, f32[8,256]{1,0:T(8,128)} %bitcast.3, s32[1,32]{1,0:T(1,128)} %refs_2_.1, bf16[256,1024]{1,0:T(8,128)(2,1)} %refs_3_.1, bf16[1,1024,512]{2,1,0:T(8,128)(2,1)} %refs_4_.1, bf16[1,1024,512]{2,1,0:T(8,128)(2,1)} %refs_5_.1, bf16[1,512,1024]{2,1,0:T(8,128)(2,1)} %refs_6_.1), custom_call_target="tpu_custom_call" | custom-call | tf_op jit(solution)/shard_map/moe_kernel/pallas_call | solution.py:336
  129.1 0.8 copy.9
